TPU v7x, 256 devices: a whole 4x4x8 slice. The times are simulated.
256 devices in a mesh: dp: 8 (over x, core), expert: 32 (over y, z).
Axes of the slice: x: 4, y: 4, z: 8, core: 2. Of those that a mesh axis runs over, the one named last changes fastest.
Arguments:
- queries: bfloat16 [2048, 16, 3072], P('expert', 'dp'), may hold values from -256 to 256
- key_nope: bfloat16 [2048, 16, 2048], P('expert', 'dp'), may hold values from -4 to 4
- key_rope: bfloat16 [2048, 16, 64], P('expert', 'dp'), may hold values from -4 to 4
- values: bfloat16 [2048, 16, 2048], P('expert', 'dp'), may hold values from -6 to 6
- residual: bfloat16 [2048, 16, 2048], P('expert', 'dp'), may hold values from -6 to 6
- segments: int32 [16, 2048], P('dp'), may hold values from 0 to 1, never falling along the last dimension, each value on 1 to 1536 neighbouring positions
- out_proj: bfloat16 [2048, 2048], P(('dp', 'expert')), may hold values from -0.125 to 0.125
- norm_gain: bfloat16 [2048], replicated, may hold values from 0.5 to 1.5
- expert_gate: bfloat16 [32, 2048, 704], P('expert'), may hold values from -0.125 to 0.125
- expert_up: bfloat16 [32, 2048, 704], P('expert'), may hold values from -0.125 to 0.125
- expert_down: bfloat16 [32, 704, 2048], P('expert'), may hold values from -0.21875 to 0.21875
- routes: int32 [8, 32, 128, 6], P('dp', 'expert'), may hold values from 0 to 31, all different within a row; in each aligned block of 128 rows (0 to 127, 128 to 255, ..., all dimensions but the last counted through in order) at most 36 rows name the same one
- route_weights: float32 [8, 32, 128, 6], P('dp', 'expert'), may hold values from 0.1 to 0.6
Outputs:
- layer_out: bfloat16 [2048, 16, 2048], P('expert', 'dp')
Inputs may be any that keep to these rules, and one draw needn't show every extreme that they name: `routes`: each row names 6 different experts; within the rows of one device no expert is named more than 36 times.
All inputs are finite; a program needn't handle non-finite values.
Results may differ from a plain program's by a relative error of at most 0.0049.
Values may be sent and summed in bfloat16 or wider, within the bound.
No kernel may reach another device: no remote copies, remote signals or barrier semaphores. Data moves between devices by JAX's collectives and lax.ppermute only.
A program may use at most 128 MiB of HBM per device.

v0:
```python
import jax
import jax.numpy as jnp
from jax import lax
from jax.sharding import PartitionSpec as P

HEADS = 16
NOPE = 128
ROPE = 64
V_DIM = 128
TOP = 6
EPSILON = 1e-06
QUERY_BLOCK = 512


def side_by_side(arrays, axis, split_dim, concat_dim, along):
    widths = [a.shape[along] for a in arrays]
    both = jnp.concatenate(arrays, axis=along)
    result = lax.all_to_all(both, axis, split_axis=split_dim, concat_axis=concat_dim, tiled=True)
    return tuple(jnp.split(result, [sum(widths[:k]) for k in range(1, len(widths))], axis=along))


def feed_forward(rows, gate_matrix, up_matrix, down_matrix):
    gate_part = jnp.dot(rows, gate_matrix, preferred_element_type=jnp.float32)
    up_part = jnp.dot(rows, up_matrix, preferred_element_type=jnp.float32)
    activated = (jax.nn.silu(gate_part) * up_part).astype(jnp.bfloat16)
    return jnp.dot(activated, down_matrix, preferred_element_type=jnp.float32).astype(jnp.bfloat16)


def attend_items(query_items, key_items, value_items, segment_items):
    length, count_items, qk_width = query_items.shape
    block_rows = QUERY_BLOCK
    score_scale = qk_width ** (-0.5)
    key_positions = jnp.arange(length, dtype=jnp.int32)

    def one_block(block_index):
        first_row = block_index * block_rows
        query_block = lax.dynamic_slice_in_dim(query_items, first_row, block_rows, 0)
        scores = (
            jnp.einsum("qid,kid->iqk", query_block, key_items, preferred_element_type=jnp.float32)
            * score_scale
        )
        row_positions = first_row + jnp.arange(block_rows, dtype=jnp.int32)
        row_segments = lax.dynamic_slice_in_dim(segment_items, first_row, block_rows, 1)
        allowed = (row_positions[None, :, None] >= key_positions[None, None, :]) & (
            row_segments[:, :, None] == segment_items[:, None, :]
        )
        scores = jnp.where(allowed, scores, -jnp.inf)
        row_peak = jnp.max(scores, axis=2, keepdims=True)
        raised = jnp.exp(scores - row_peak)
        weights = (raised / jnp.sum(raised, axis=2, keepdims=True)).astype(jnp.bfloat16)
        return jnp.einsum(
            "iqk,kid->qid", weights, value_items, preferred_element_type=jnp.float32
        ).astype(jnp.bfloat16)

    blocks = lax.map(one_block, jnp.arange(length // block_rows, dtype=jnp.int32))
    return blocks.reshape(length, count_items, value_items.shape[2])


def body(
    queries,
    key_nope,
    key_rope,
    values,
    residual,
    segments,
    out_proj,
    norm_gain,
    expert_gate,
    expert_up,
    expert_down,
    routes,
    route_weights,
):
    half_rows, stream_count, query_width = queries.shape
    model_width = residual.shape[2]
    token_rows = half_rows * stream_count
    pair_count = token_rows * TOP
    expert_count = lax.axis_size("expert")
    item_count = stream_count * HEADS // expert_count
    key_heads = jnp.concatenate(
        [
            key_nope.reshape(half_rows, stream_count, HEADS, NOPE),
            jnp.broadcast_to(key_rope[:, :, None, :], (half_rows, stream_count, HEADS, ROPE)),
        ],
        axis=3,
    )
    query_items = queries.reshape(half_rows, stream_count * HEADS, NOPE + ROPE)
    key_items = key_heads.reshape(half_rows, stream_count * HEADS, NOPE + ROPE)
    value_items = values.reshape(half_rows, stream_count * HEADS, V_DIM)
    query_all, key_all, value_all = side_by_side(
        (query_items, key_items, value_items), "expert", 1, 0, 2
    )
    item_ids = lax.axis_index("expert") * item_count + jnp.arange(item_count, dtype=jnp.int32)
    stream_ids = item_ids // HEADS
    selector = (stream_ids[:, None] == jnp.arange(stream_count, dtype=jnp.int32)[None, :]).astype(
        jnp.int32
    )
    segment_items = jnp.sum(selector[:, :, None] * segments[None, :, :], axis=1)
    attended_items = attend_items(query_all, key_all, value_all, segment_items)
    attended_back = lax.all_to_all(
        attended_items, "expert", split_axis=0, concat_axis=1, tiled=True
    )
    attn_rows = attended_back.reshape(token_rows, HEADS * V_DIM)
    projected = jnp.dot(
        attn_rows,
        lax.all_gather(out_proj, ("dp", "expert"), axis=0, tiled=True),
        preferred_element_type=jnp.float32,
    )
    hidden = residual.reshape(token_rows, model_width).astype(jnp.float32) + projected
    mean_square = jnp.mean(hidden * hidden, axis=1, keepdims=True)
    normed = (hidden * lax.rsqrt(mean_square + EPSILON) * norm_gain.astype(jnp.float32)).astype(
        jnp.bfloat16
    )
    capacity = min(token_rows, max(2, token_rows * TOP * 3 // (2 * expert_count)))
    flat_routes = routes.reshape(pair_count)
    matches = (flat_routes[:, None] == jnp.arange(expert_count, dtype=jnp.int32)[None, :]).astype(
        jnp.int32
    )
    earlier = jnp.cumsum(matches, axis=0) - matches
    slot_rank = jnp.sum(earlier * matches, axis=1)
    target = flat_routes * capacity + slot_rank
    pair_ids = jnp.arange(pair_count, dtype=jnp.int32)
    slot_source = (
        jnp.full((expert_count * capacity,), pair_count, jnp.int32).at[target].set(pair_ids)
    )
    slot_live = slot_source < pair_count
    slot_rows = normed[jnp.minimum(slot_source, pair_count - 1) // TOP]
    outgoing = jnp.where(slot_live[:, None], slot_rows, jnp.zeros_like(slot_rows)).reshape(
        expert_count, capacity, model_width
    )
    gate_matrix = expert_gate[0]
    up_matrix = expert_up[0]
    down_matrix = expert_down[0]
    arrived = lax.all_to_all(outgoing, "expert", split_axis=0, concat_axis=0, tiled=True)
    source_count, slot_count, width = arrived.shape
    flat_rows = arrived.reshape(source_count * slot_count, width)
    results = feed_forward(flat_rows, gate_matrix, up_matrix, down_matrix)
    returned = lax.all_to_all(
        results.reshape(source_count, slot_count, width),
        "expert",
        split_axis=0,
        concat_axis=0,
        tiled=True,
    )
    pair_outputs = returned.reshape(expert_count * capacity, model_width)[target]
    weighted = route_weights.reshape(pair_count, 1) * pair_outputs.astype(jnp.float32)
    routed_sum = jnp.sum(weighted.reshape(token_rows, TOP, model_width), axis=1)
    layer_out = (hidden + routed_sum).astype(jnp.bfloat16)
    return layer_out.reshape(half_rows, stream_count, model_width)


def solution(mesh):
    return jax.shard_map(
        body,
        mesh=mesh,
        in_specs=(
            P("expert", "dp", None),
            P("expert", "dp", None),
            P("expert", "dp", None),
            P("expert", "dp", None),
            P("expert", "dp", None),
            P("dp", None),
            P(("dp", "expert"), None),
            P(),
            P("expert", None, None),
            P("expert", None, None),
            P("expert", None, None),
            P("dp", "expert", None, None),
            P("dp", "expert", None, None),
        ),
        out_specs=P("expert", "dp", None),
        check_vma=False,
    )
```

profile of v0, /device:TPU:2, one launch (start us, length us, event | category | flops | bytes accessed | tf_op | source)
XLA Modules:
  0.0 490.3 jit_solution(3616979973672763825)
XLA Ops:
  7.3 3.5 reshape.177
  10.8 1.4 concatenate.10
  12.2 2.2 reshape.178
  15.2 2.3 pad_maximum_fusion
  17.5 2.6 copy.45
  20.1 11.7 %all-to-all-start = ((bf16[64,32,512]{2,0,1:T(8,128)(2,1)}), bf16[64,32,512]{2,0,1:T(8,128)(2,1)}, u32[]{:S(2)}, u32[]{:S(2)}) async-start(bf16[64,32,512]{2,0,1:T(8,128)(2,1)} %copy.45), calls=%async_computation | async-start | bytes 4194304 | tf_op jit(solution)/shard_map/all_to_all | solution.py:18
  32.3 1.2 reshape.186
  33.5 1.7 reduce-window.6
  35.7 49.4 %all-to-all-done = bf16[64,32,512]{2,0,1:T(8,128)(2,1)} async-done(((bf16[64,32,512]{2,0,1:T(8,128)(2,1)}), bf16[64,32,512]{2,0,1:T(8,128)(2,1)}, u32[]{:S(2)}, u32[]{:S(2)}) %all-to-all-start) | async-done | bytes 2097184 | tf_op jit(solution)/shard_map/all_to_all | solution.py:18
  85.0 1.1 split.14
  86.1 3.6 fusion.27
  89.7 2.2 copy.46
  91.9 2.2 copy.47
  94.1 24.3 %while.11 = (s32[]{:T(128)}, bf16[4,512,1,128]{3,1,2,0:T(8,128)(2,1)}, s32[4]{0:T(128)S(1)}, s32[1,2048]{1,0:T(1,128)S(1)}, bf16[2048,1,192]{0,2,1:T(8,128)(2,1)...) while((s32[]{:T(128)}, ...), condition=%wide.region_4.5_spmd.clone, body=%wide.region_1.4_spmd.clone.sunk | while | flops 682688000 | bytes 14250675 | solution.py:55
  95.4 2.6 fusion.38
  98.7 1.5 fusion.40
  101.4 2.6 fusion.38
  104.7 1.5 fusion.40
  107.5 2.6 fusion.38
  110.8 1.5 fusion.40
  113.6 2.6 fusion.38
  116.9 1.5 fusion.40
  119.0 2.1 reduce.10
  122.0 5.5 %all-to-all-start.1 = ((bf16[32,2,4096]{2,1,0:T(2,128)(2,1)}), bf16[32,2,4096]{2,1,0:T(2,128)(2,1)S(1)}, u32[]{:S(2)}, u32[]{:S(2)}) async-start(bf16[32,2,4096]{2,1,0:T(2,128)(2,1)} %reshape.220), calls=%async_computation.1 | async-start | bytes 1048576 | tf_op jit(solution)/shard_map/all_to_all | solution.py:100
  129.4 3.6 scatter_custom_fusion
  133.1 11.8 %all-to-all-done.1 = bf16[32,2,4096]{2,1,0:T(2,128)(2,1)S(1)} async-done(((bf16[32,2,4096]{2,1,0:T(2,128)(2,1)}), bf16[32,2,4096]{2,1,0:T(2,128)(2,1)S(1)}, u32[]{:S(2)}, u32[]{:S(2)}) %all-to-all-start.1) | async-done | bytes 524320 | tf_op jit(solution)/shard_map/all_to_all | solution.py:100
  144.9 1.8 reshape.221
  146.7 1.3 copy.56
  148.0 1.1 copy.49
  149.2 1.3 reshape.180
  150.5 5.0 %multiply_reduce_fusion.1 = (f32[128]{0:T(128)S(1)}, f32[128,2048]{1,0:T(8,128)S(1)}) fusion(f32[128,2048]{1,0:T(8,128)} %reshape.186, bf16[128,2048]{1,0:T(8,128)(2,1)S(1)} %reshape.180, bf16[2048,2048]{1,0:T(8,128)(2,1)} %all-gather.2.cloned.1.call-done), kind=kOutput, calls=%fused_computation.34 | convolution fusion | flops 1074528128 | bytes 11010560 | tf_op jit(solution)/shard_map/dot_general | solution.py:104
  155.5 1.0 copy-done.1
  156.6 6.1 %gather_fusion = bf16[1152,2048]{1,0:T(8,128)(2,1)} fusion(bf16[128,2048]{1,0:T(8,128)(2,1)S(1)} %multiply_convert_fusion, s32[2048]{0:T(1024)S(1)} %pad_clamp_fusion), kind=kCustom, calls=%fused_computation | custom fusion | bytes 9441792 | tf_op jit(solution)/shard_map/gather | solution.py:127
  162.7 7.2 %gather.9 = bf16[32,36,2048]{2,1,0:T(8,128)(2,1)} reshape(bf16[1152,2048]{1,0:T(8,128)(2,1)} %gather_fusion) | data formatting | bytes 9437184 | tf_op jit(solution)/shard_map/gather | solution.py:127
  169.9 2.9 broadcast_select_fusion
  172.8 123.9 %all_to_all.43 = bf16[32,36,2048]{2,1,0:T(8,128)(2,1)} all-to-all(bf16[32,36,2048]{2,1,0:T(8,128)(2,1)S(1)} %broadcast_select_fusion), channel_id=1, replica_groups=mesh['dp'=8,'expert'=32] {'expert'}, dimensions={0} | all-to-all | bytes 9437184 | tf_op jit(solution)/shard_map/all_to_all | solution.py:134
  296.7 7.3 %reshape.182 = bf16[1152,2048]{1,0:T(8,128)(2,1)} reshape(bf16[32,36,2048]{2,1,0:T(8,128)(2,1)} %all_to_all.43) | data formatting | bytes 9437184 | tf_op jit(solution)/shard_map/reshape | solution.py:136
  304.0 7.3 %fusion.16 = f32[1152,704]{0,1:T(8,128)S(1)} fusion(bf16[1152,2048]{1,0:T(8,128)(2,1)} %reshape.182, bf16[1,2048,704]{1,2,0:T(8,128)(2,1)} %param.23), kind=kOutput, calls=%fused_computation.28 | convolution fusion | flops 3321888768 | bytes 10846208 | tf_op jit(solution)/shard_map/dot_general | solution.py:23
  311.3 4.0 fusion.13
  315.4 5.6 %convolution_convert_fusion = bf16[1152,2048]{1,0:T(8,128)(2,1)} fusion(bf16[1152,704]{0,1:T(8,128)(2,1)S(1)} %fusion.13, bf16[1,704,2048]{2,1,0:T(8,128)(2,1)S(1)} %copy-done), kind=kOutput, calls=%fused_computation.22 | convolution fusion | flops 3324248064 | bytes 9224192 | tf_op jit(solution)/shard_map/dot_general | solution.py:26
  320.9 7.3 %reshape.183 = bf16[32,36,2048]{2,1,0:T(8,128)(2,1)} reshape(bf16[1152,2048]{1,0:T(8,128)(2,1)} %convolution_convert_fusion) | data formatting | bytes 9437184 | tf_op jit(solution)/shard_map/reshape | solution.py:139
  328.2 5.4 %all-to-all-start.3 = ((bf16[32,36,2048]{2,1,0:T(8,128)(2,1)}), bf16[32,36,2048]{2,1,0:T(8,128)(2,1)}, u32[]{:S(2)}, u32[]{:S(2)}) async-start(bf16[32,36,2048]{2,1,0:T(8,128)(2,1)} %reshape.183), calls=%async_computation.3 | async-start | bytes 10485760 | tf_op jit(solution)/shard_map/all_to_all | solution.py:138
  333.7 117.9 %all-to-all-done.3 = bf16[32,36,2048]{2,1,0:T(8,128)(2,1)} async-done(((bf16[32,36,2048]{2,1,0:T(8,128)(2,1)}), bf16[32,36,2048]{2,1,0:T(8,128)(2,1)}, u32[]{:S(2)}, u32[]{:S(2)}) %all-to-all-start.3) | async-done | bytes 4718624 | tf_op jit(solution)/shard_map/all_to_all | solution.py:138
  451.6 7.3 %reshape.184 = bf16[1152,2048]{1,0:T(8,128)(2,1)} reshape(bf16[32,36,2048]{2,1,0:T(8,128)(2,1)} %all-to-all-done.3) | data formatting | bytes 9437184 | tf_op jit(solution)/shard_map/reshape | solution.py:145
  458.9 10.0 %gather_fusion.1 = bf16[768,2048]{1,0:T(8,128)(2,1)} fusion(bf16[1152,2048]{1,0:T(8,128)(2,1)} %reshape.184, s32[1024]{0:T(1024)S(1)} %pad_clamp_fusion.1), kind=kCustom, calls=%fused_computation.1 | custom fusion | bytes 6294528 | tf_op jit(solution)/shard_map/gather | solution.py:145
  469.0 6.5 %reshape.187 = f32[128,6,2048]{2,1,0:T(8,128)} reshape(bf16[768,2048]{1,0:T(8,128)(2,1)} %gather_fusion.1) | data formatting | bytes 9437184 | tf_op jit(solution)/shard_map/convert_element_type | solution.py:146
  475.5 6.7 %multiply_reduce_fusion = f32[128,2048]{1,0:T(8,128)S(1)} fusion(f32[128,6,2048]{2,1,0:T(8,128)} %reshape.187, f32[128,6]{1,0:T(8,128)S(1)} %bitcast.100), kind=kLoop, calls=%fused_computation.21 | loop fusion | flops 2883584 | bytes 7343104 | tf_op jit(solution)/shard_map/reduce_sum | solution.py:147
  482.3 1.1 reshape.185
  (67 shorter events, 11.5 us)
Async XLA Ops:
  6.5 308.8 %copy-start = (bf16[1,704,2048]{2,1,0:T(8,128)(2,1)S(1)}, bf16[1,704,2048]{2,1,0:T(8,128)(2,1)}, u32[]{:S(2)}) copy-start(bf16[1,704,2048]{2,1,0:T(8,128)(2,1)} %param.25) | copy-start | bytes 8650756
  6.5 143.9 %all-gather.2.cloned.1.call-start = ((), (), s32[]{:S(2)}) async-start(), calls=%async_computation.4 | async-start | bytes 8421376 | tf_op jit(solution)/shard_map/all_gather | solution.py:106
  17.5 14.4 %copy-start.6 = (s32[1,1,128,6]{2,1,3,0:T(1,128)S(1)}, s32[1,1,128,6]{2,1,3,0:T(1,128)}, u32[]{:S(2)}) copy-start(s32[1,1,128,6]{2,1,3,0:T(1,128)} %param.26) | copy-start | bytes 9220
  17.5 14.8 %copy-start.4 = (bf16[64,2,2048]{2,1,0:T(2,128)(2,1)S(1)}, bf16[64,2,2048]{2,1,0:T(2,128)(2,1)}, u32[]{:S(2)}) copy-start(bf16[64,2,2048]{2,1,0:T(2,128)(2,1)} %param.19) | copy-start | bytes 1572868
  17.5 16.0 %copy-start.7 = (bf16[2048]{0:T(1024)(128)(2,1)S(1)}, bf16[2048]{0:T(1024)(128)(2,1)}, u32[]{:S(2)}) copy-start(bf16[2048]{0:T(1024)(128)(2,1)} %param.22) | copy-start | bytes 12292
  20.1 15.5 %copy-start.5 = (s32[2,2048]{1,0:T(2,128)S(1)}, s32[2,2048]{1,0:T(2,128)}, u32[]{:S(2)}) copy-start(s32[2,2048]{1,0:T(2,128)} %param.20) | copy-start | bytes 49156
  20.1 64.9 %all-to-all-start = ((bf16[64,32,512]{2,0,1:T(8,128)(2,1)}), bf16[64,32,512]{2,0,1:T(8,128)(2,1)}, u32[]{:S(2)}, u32[]{:S(2)}) async-start(bf16[64,32,512]{2,0,1:T(8,128)(2,1)} %copy.45), calls=%async_computation | async-start | bytes 4194304 | tf_op jit(solution)/shard_map/all_to_all | solution.py:18
  122.0 22.9 %all-to-all-start.1 = ((bf16[32,2,4096]{2,1,0:T(2,128)(2,1)}), bf16[32,2,4096]{2,1,0:T(2,128)(2,1)S(1)}, u32[]{:S(2)}, u32[]{:S(2)}) async-start(bf16[32,2,4096]{2,1,0:T(2,128)(2,1)} %reshape.220), calls=%async_computation.1 | async-start | bytes 1048576 | tf_op jit(solution)/shard_map/all_to_all | solution.py:100
  155.4 1.0 copy-start.1
  304.0 7.3 %copy-start.3 = (bf16[1152,2048]{1,0:T(8,128)(2,1)S(1)}, bf16[1152,2048]{1,0:T(8,128)(2,1)}, u32[]{:S(2)}) copy-start(bf16[1152,2048]{1,0:T(8,128)(2,1)} %reshape.182) | copy-start | bytes 14155780
  304.0 7.3 %copy-start.9 = (bf16[1,2048,704]{1,2,0:T(8,128)(2,1)S(1)}, bf16[1,2048,704]{1,2,0:T(8,128)(2,1)}, u32[]{:S(2)}) copy-start(bf16[1,2048,704]{1,2,0:T(8,128)(2,1)} %param.24) | copy-start | bytes 8650756
  328.2 5.4 %copy-start.8 = (f32[1,1,128,6]{2,1,3,0:T(1,128)S(1)}, f32[1,1,128,6]{2,1,3,0:T(1,128)}, u32[]{:S(2)}) copy-start(f32[1,1,128,6]{2,1,3,0:T(1,128)} %param.27) | copy-start | bytes 9220
  328.2 123.4 %all-to-all-start.3 = ((bf16[32,36,2048]{2,1,0:T(8,128)(2,1)}), bf16[32,36,2048]{2,1,0:T(8,128)(2,1)}, u32[]{:S(2)}, u32[]{:S(2)}) async-start(bf16[32,36,2048]{2,1,0:T(8,128)(2,1)} %reshape.183), calls=%async_computation.3 | async-start | bytes 10485760 | tf_op jit(solution)/shard_map/all_to_all | solution.py:138
  475.5 6.7 %copy-start.2 = (f32[128,2048]{1,0:T(8,128)S(1)}, f32[128,2048]{1,0:T(8,128)}, u32[]{:S(2)}) copy-start(f32[128,2048]{1,0:T(8,128)} %copy-done.1) | copy-start | bytes 3145732
Sparse Core Ops, SparseCore 0:
  11.0 128.0 all-gather.1
where the time goes:
time: 492 us; the launch traced here: 490 us
  waiting for transfers between devices  180 us (37%)
  blocking collectives  124 us (25%)
  local copies, waits for them, and re-layouts  90.1 us (18%)
  matrix products  38.3 us (8%)
  starting transfers between devices  22.7 us (5%)
  other arithmetic  19.1 us (4%)
  between operations  13.7 us (3%)
    all_to_all x1, blocking collectives, body(): lax.all_to_all(outgoing, 'expert', split_axis=0, concat_axis=0, tiled=True)  124 us
    all_to_all x1, waiting for transfers between devices, body(): lax.all_to_all(results.reshape(source_count, slot_count, width), 'expert'...  118 us
    all_to_all x1, waiting for transfers between devices, side_by_side(): lax.all_to_all(both, axis, split_axis=split_dim, concat_axis=concat_dim,...  49.4 us
    gather x2, local copies, waits for them, and re-layouts, body(): slot_rows = normed[jnp.minimum(slot_source, pair_count - 1) // TOP]  13.3 us
    all_to_all x1, waiting for transfers between devices, body(): lax.all_to_all(attended_items, 'expert', split_axis=0, concat_axis=1, til...  11.8 us
    all_to_all x1, starting transfers between devices, side_by_side(): lax.all_to_all(both, axis, split_axis=split_dim, concat_axis=concat_dim,...  11.7 us
    dot_general x4, matrix products, one_block(): jnp.einsum('qid,kid->iqk', query_block, key_items, preferred_element_type...  10.3 us
    gather x1, local copies, waits for them, and re-layouts, body(): returned.reshape(expert_count * capacity, model_width)[target]  10 us
  transfers between devices with their start and end apart: 4, of which 3 were waited for; matrix products, arithmetic and copies ran while one was open for 13% of the time, Pallas kernels for 0%

commit v1 on v0

--- a/solution.py
+++ b/solution.py
@@ -97,8 +97,11 @@
     )
     segment_items = jnp.sum(selector[:, :, None] * segments[None, :, :], axis=1)
     attended_items = attend_items(query_all, key_all, value_all, segment_items)
-    attended_back = lax.all_to_all(
-        attended_items, "expert", split_axis=0, concat_axis=1, tiled=True
+    attended_back = jnp.concatenate(
+        lax.all_to_all(
+            jnp.stack(jnp.split(attended_items, lax.axis_size("expert"), axis=0)), "expert", 0, 0
+        ),
+        axis=1,
     )
     attn_rows = attended_back.reshape(token_rows, HEADS * V_DIM)
     projected = jnp.dot(

time: 492 us -> 506 us (1.028)
  local copies, waits for them, and re-layouts: 90.1 us -> 107 us
    unnamed x26 -> x56, local copies, waits for them, and re-layouts: 9.58 us -> 24.4 us
  transfers between devices with their start and end apart: 4 -> 4, of which waited for: 3 -> 3; matrix products, arithmetic and copies ran while one was open for 13% -> 12% of each run, Pallas kernels for 0% -> 0%
where the time goes in v1:
time: 506 us; the launch traced here: 503 us
  waiting for transfers between devices  180 us (36%)
  blocking collectives  124 us (25%)
  local copies, waits for them, and re-layouts  107 us (21%)
  matrix products  35.9 us (7%)
  starting transfers between devices  23.3 us (5%)
  other arithmetic  17 us (3%)
  between operations  13.8 us (3%)
    all_to_all x1, blocking collectives, body(): lax.all_to_all(outgoing, 'expert', split_axis=0, concat_axis=0, tiled=True)  124 us
    all_to_all x1, waiting for transfers between devices, body(): lax.all_to_all(results.reshape(source_count, slot_count, width), 'expert'...  118 us
    all_to_all x1, waiting for transfers between devices, side_by_side(): lax.all_to_all(both, axis, split_axis=split_dim, concat_axis=concat_dim,...  46.2 us
    unnamed x56, local copies, waits for them, and re-layouts  24.4 us
    all_to_all x1, waiting for transfers between devices, body(): lax.all_to_all(jnp.stack(jnp.split(attended_items, lax.axis_size('expert'...  15 us
    gather x2, local copies, waits for them, and re-layouts, body(): slot_rows = normed[jnp.minimum(slot_source, pair_count - 1) // TOP]  13.2 us
    all_to_all x1, starting transfers between devices, side_by_side(): lax.all_to_all(both, axis, split_axis=split_dim, concat_axis=concat_dim,...  11.7 us
    dot_general x4, matrix products, one_block(): jnp.einsum('qid,kid->iqk', query_block, key_items, preferred_element_type...  10.3 us
  transfers between devices with their start and end apart: 4, of which 3 were waited for; matrix products, arithmetic and copies ran while one was open for 12% of the time, Pallas kernels for 0%

profile of v1, /device:TPU:2, one launch (start us, length us, event | category | flops | bytes accessed | tf_op | source)
XLA Modules:
  0.0 503.4 jit_solution(4057200673317772792)
XLA Ops:
  6.5 3.5 reshape.176
  10.0 1.4 concatenate.10
  11.4 2.2 reshape.177
  13.6 0.8 broadcast_in_dim.30
  14.4 2.3 pad_maximum_fusion
  16.8 2.5 copy.67
  19.2 11.7 %all-to-all-start = ((bf16[64,32,512]{2,0,1:T(8,128)(2,1)}), bf16[64,32,512]{2,0,1:T(8,128)(2,1)}, u32[]{:S(2)}, u32[]{:S(2)}) async-start(bf16[64,32,512]{2,0,1:T(8,128)(2,1)} %copy.67), calls=%async_computation | async-start | bytes 4194304 | tf_op jit(solution)/shard_map/all_to_all | solution.py:18
  32.1 1.2 reshape.185
  33.4 1.7 reduce-window.6
  35.5 46.2 %all-to-all-done = bf16[64,32,512]{2,0,1:T(8,128)(2,1)} async-done(((bf16[64,32,512]{2,0,1:T(8,128)(2,1)}), bf16[64,32,512]{2,0,1:T(8,128)(2,1)}, u32[]{:S(2)}, u32[]{:S(2)}) %all-to-all-start) | async-done | bytes 2097184 | tf_op jit(solution)/shard_map/all_to_all | solution.py:18
  81.8 1.9 split.142
  83.6 3.5 fusion.27
  87.1 2.3 copy.68
  89.4 2.2 copy.69
  91.6 23.3 %while.11 = (s32[]{:T(128)}, bf16[4,512,1,128]{3,1,2,0:T(8,128)(2,1)S(1)}, s32[4]{0:T(128)S(1)}, s32[1,2048]{1,0:T(1,128)S(1)}, bf16[2048,1,192]{0,2,1:T(8,128)(...) while((s32[]{:T(128)}, ...), condition=%wide.region_4.5_spmd.clone, body=%wide.region_1.4_spmd.clone.sunk | while | flops 682688000 | bytes 16347347 | solution.py:55
  92.8 2.6 fusion.38
  96.5 0.9 fusion.40
  98.7 2.6 fusion.38
  102.3 0.9 fusion.40
  104.5 2.6 fusion.38
  108.2 0.9 fusion.40
  110.4 2.6 fusion.38
  114.0 0.9 fusion.40
  134.4 6.1 %all-to-all-start.1 = ((bf16[32,64,1,128]{3,1,2,0:T(8,128)(2,1)}), bf16[32,64,1,128]{3,1,2,0:T(8,128)(2,1)S(1)}, u32[]{:S(2)}, u32[]{:S(2)}) async-start(bf16[32,64,1,128]{3,1,2,0:T(8,128)(2,1)} %constant_dynamic-update-slice_fusion), calls=%async_computation.1 | async-start | bytes 1048576 | tf_op jit(solution)/shard_map/all_to_all | solution.py:101
  140.4 0.7 copy.72
  141.2 1.0 mul.81
  142.3 3.6 scatter_custom_fusion
  146.0 15.0 %all-to-all-done.1 = bf16[32,64,1,128]{3,1,2,0:T(8,128)(2,1)S(1)} async-done(((bf16[32,64,1,128]{3,1,2,0:T(8,128)(2,1)}), bf16[32,64,1,128]{3,1,2,0:T(8,128)(2,1)S(1)}, u32[]{:S(2)}, u32[]{:S(2)}) %all-to-all-start.1) | async-done | bytes 524320 | tf_op jit(solution)/shard_map/all_to_all | solution.py:101
  161.0 1.1 copy.70
  162.2 1.3 reshape_reshape.3
  163.5 5.0 multiply_reduce_fusion.1
  168.5 1.0 copy-done.1
  169.6 6.0 %gather_fusion = bf16[1152,2048]{1,0:T(8,128)(2,1)} fusion(bf16[128,2048]{1,0:T(8,128)(2,1)S(1)} %multiply_convert_fusion, s32[2048]{0:T(1024)S(1)} %pad_clamp_fusion), kind=kCustom, calls=%fused_computation | custom fusion | bytes 9441792 | tf_op jit(solution)/shard_map/gather | solution.py:130
  175.6 7.2 %gather.9 = bf16[32,36,2048]{2,1,0:T(8,128)(2,1)} reshape(bf16[1152,2048]{1,0:T(8,128)(2,1)} %gather_fusion) | data formatting | bytes 9437184 | tf_op jit(solution)/shard_map/gather | solution.py:130
  182.8 2.9 broadcast_select_fusion
  185.7 124.3 %all_to_all.33 = bf16[32,36,2048]{2,1,0:T(8,128)(2,1)} all-to-all(bf16[32,36,2048]{2,1,0:T(8,128)(2,1)S(1)} %broadcast_select_fusion), channel_id=1, replica_groups=mesh['dp'=8,'expert'=32] {'expert'}, dimensions={0} | all-to-all | bytes 9437184 | tf_op jit(solution)/shard_map/all_to_all | solution.py:137
  310.0 7.2 %reshape.181 = bf16[1152,2048]{1,0:T(8,128)(2,1)} reshape(bf16[32,36,2048]{2,1,0:T(8,128)(2,1)} %all_to_all.33) | data formatting | bytes 9437184 | tf_op jit(solution)/shard_map/reshape | solution.py:139
  317.2 7.3 %fusion.16 = f32[1152,704]{0,1:T(8,128)S(1)} fusion(bf16[1152,2048]{1,0:T(8,128)(2,1)} %reshape.181, bf16[1,2048,704]{1,2,0:T(8,128)(2,1)} %param.23), kind=kOutput, calls=%fused_computation.28 | convolution fusion | flops 3321888768 | bytes 10846208 | tf_op jit(solution)/shard_map/dot_general | solution.py:23
  324.5 4.0 fusion.13
  328.5 5.6 %convolution_convert_fusion = bf16[1152,2048]{1,0:T(8,128)(2,1)} fusion(bf16[1152,704]{0,1:T(8,128)(2,1)S(1)} %fusion.13, bf16[1,704,2048]{2,1,0:T(8,128)(2,1)S(1)} %copy-done), kind=kOutput, calls=%fused_computation.22 | convolution fusion | flops 3324248064 | bytes 9224192 | tf_op jit(solution)/shard_map/dot_general | solution.py:26
  334.1 7.2 %reshape.182 = bf16[32,36,2048]{2,1,0:T(8,128)(2,1)} reshape(bf16[1152,2048]{1,0:T(8,128)(2,1)} %convolution_convert_fusion) | data formatting | bytes 9437184 | tf_op jit(solution)/shard_map/reshape | solution.py:142
  341.3 5.4 %all-to-all-start.3 = ((bf16[32,36,2048]{2,1,0:T(8,128)(2,1)}), bf16[32,36,2048]{2,1,0:T(8,128)(2,1)}, u32[]{:S(2)}, u32[]{:S(2)}) async-start(bf16[32,36,2048]{2,1,0:T(8,128)(2,1)} %reshape.182), calls=%async_computation.3 | async-start | bytes 10485760 | tf_op jit(solution)/shard_map/all_to_all | solution.py:141
  346.9 117.9 %all-to-all-done.3 = bf16[32,36,2048]{2,1,0:T(8,128)(2,1)} async-done(((bf16[32,36,2048]{2,1,0:T(8,128)(2,1)}), bf16[32,36,2048]{2,1,0:T(8,128)(2,1)}, u32[]{:S(2)}, u32[]{:S(2)}) %all-to-all-start.3) | async-done | bytes 4718624 | tf_op jit(solution)/shard_map/all_to_all | solution.py:141
  464.7 7.2 %reshape.183 = bf16[1152,2048]{1,0:T(8,128)(2,1)} reshape(bf16[32,36,2048]{2,1,0:T(8,128)(2,1)} %all-to-all-done.3) | data formatting | bytes 9437184 | tf_op jit(solution)/shard_map/reshape | solution.py:148
  471.9 10.1 %gather_fusion.1 = bf16[768,2048]{1,0:T(8,128)(2,1)} fusion(bf16[1152,2048]{1,0:T(8,128)(2,1)} %reshape.183, s32[1024]{0:T(1024)S(1)} %pad_clamp_fusion.1), kind=kCustom, calls=%fused_computation.1 | custom fusion | bytes 6294528 | tf_op jit(solution)/shard_map/gather | solution.py:148
  482.0 6.6 %reshape.186 = f32[128,6,2048]{2,1,0:T(8,128)} reshape(bf16[768,2048]{1,0:T(8,128)(2,1)} %gather_fusion.1) | data formatting | bytes 9437184 | tf_op jit(solution)/shard_map/convert_element_type | solution.py:149
  488.6 6.7 %multiply_reduce_fusion = f32[128,2048]{1,0:T(8,128)S(1)} fusion(f32[128,6,2048]{2,1,0:T(8,128)} %reshape.186, f32[128,6]{1,0:T(8,128)S(1)} %bitcast.258), kind=kLoop, calls=%fused_computation.21 | loop fusion | flops 2883584 | bytes 7343104 | tf_op jit(solution)/shard_map/reduce_sum | solution.py:150
  495.4 1.1 reshape.184
  (104 shorter events, 28.2 us)
Async XLA Ops:
  6.5 322.0 %copy-start = (bf16[1,704,2048]{2,1,0:T(8,128)(2,1)S(1)}, bf16[1,704,2048]{2,1,0:T(8,128)(2,1)}, u32[]{:S(2)}) copy-start(bf16[1,704,2048]{2,1,0:T(8,128)(2,1)} %param.25) | copy-start | bytes 8650756
  16.7 15.0 %copy-start.8 = (s32[1,1,128,6]{2,1,3,0:T(1,128)S(1)}, s32[1,1,128,6]{2,1,3,0:T(1,128)}, u32[]{:S(2)}) copy-start(s32[1,1,128,6]{2,1,3,0:T(1,128)} %param.26) | copy-start | bytes 9220
  16.7 15.4 %copy-start.4 = (bf16[64,2,2048]{2,1,0:T(2,128)(2,1)S(1)}, bf16[64,2,2048]{2,1,0:T(2,128)(2,1)}, u32[]{:S(2)}) copy-start(bf16[64,2,2048]{2,1,0:T(2,128)(2,1)} %param.19) | copy-start | bytes 1572868
  16.7 16.6 %copy-start.9 = (bf16[2048]{0:T(1024)(128)(2,1)S(1)}, bf16[2048]{0:T(1024)(128)(2,1)}, u32[]{:S(2)}) copy-start(bf16[2048]{0:T(1024)(128)(2,1)} %param.22) | copy-start | bytes 12292
  19.2 16.2 %copy-start.7 = (s32[2,2048]{1,0:T(2,128)S(1)}, s32[2,2048]{1,0:T(2,128)}, u32[]{:S(2)}) copy-start(s32[2,2048]{1,0:T(2,128)} %param.20) | copy-start | bytes 49156
  19.2 62.5 %all-to-all-start = ((bf16[64,32,512]{2,0,1:T(8,128)(2,1)}), bf16[64,32,512]{2,0,1:T(8,128)(2,1)}, u32[]{:S(2)}, u32[]{:S(2)}) async-start(bf16[64,32,512]{2,0,1:T(8,128)(2,1)} %copy.67), calls=%async_computation | async-start | bytes 4194304 | tf_op jit(solution)/shard_map/all_to_all | solution.py:18
  31.0 132.5 %all-gather.2.cloned.1.call-start = ((), (), s32[]{:S(2)}) async-start(), calls=%async_computation.4 | async-start | bytes 8421376 | tf_op jit(solution)/shard_map/all_gather | solution.py:109
  83.6 8.0 %copy-start.5 = (bf16[4,512,1,128]{3,1,2,0:T(8,128)(2,1)S(1)}, bf16[4,512,1,128]{3,1,2,0:T(8,128)(2,1)}, u32[]{:S(2)}) copy-start(bf16[4,512,1,128]{3,1,2,0:T(8,128)(2,1)} %custom-call.5) | copy-start | bytes 1572868
  95.5 1.0 copy-start.6
  101.3 1.1 copy-start.6
  107.1 1.0 copy-start.6
  113.0 1.0 copy-start.6
  134.4 26.7 %all-to-all-start.1 = ((bf16[32,64,1,128]{3,1,2,0:T(8,128)(2,1)}), bf16[32,64,1,128]{3,1,2,0:T(8,128)(2,1)S(1)}, u32[]{:S(2)}, u32[]{:S(2)}) async-start(bf16[32,64,1,128]{3,1,2,0:T(8,128)(2,1)} %constant_dynamic-update-slice_fusion), calls=%async_computation.1 | async-start | bytes 1048576 | tf_op jit(solution)/shard_map/all_to_all | solution.py:101
  168.5 1.0 copy-start.1
  317.2 7.3 %copy-start.3 = (bf16[1152,2048]{1,0:T(8,128)(2,1)S(1)}, bf16[1152,2048]{1,0:T(8,128)(2,1)}, u32[]{:S(2)}) copy-start(bf16[1152,2048]{1,0:T(8,128)(2,1)} %reshape.181) | copy-start | bytes 14155780
  317.2 7.3 %copy-start.11 = (bf16[1,2048,704]{1,2,0:T(8,128)(2,1)S(1)}, bf16[1,2048,704]{1,2,0:T(8,128)(2,1)}, u32[]{:S(2)}) copy-start(bf16[1,2048,704]{1,2,0:T(8,128)(2,1)} %param.24) | copy-start | bytes 8650756
  341.3 5.4 %copy-start.10 = (f32[1,1,128,6]{2,1,3,0:T(1,128)S(1)}, f32[1,1,128,6]{2,1,3,0:T(1,128)}, u32[]{:S(2)}) copy-start(f32[1,1,128,6]{2,1,3,0:T(1,128)} %param.27) | copy-start | bytes 9220
  341.3 123.4 %all-to-all-start.3 = ((bf16[32,36,2048]{2,1,0:T(8,128)(2,1)}), bf16[32,36,2048]{2,1,0:T(8,128)(2,1)}, u32[]{:S(2)}, u32[]{:S(2)}) async-start(bf16[32,36,2048]{2,1,0:T(8,128)(2,1)} %reshape.182), calls=%async_computation.3 | async-start | bytes 10485760 | tf_op jit(solution)/shard_map/all_to_all | solution.py:141
  488.6 6.7 %copy-start.2 = (f32[128,2048]{1,0:T(8,128)S(1)}, f32[128,2048]{1,0:T(8,128)}, u32[]{:S(2)}) copy-start(f32[128,2048]{1,0:T(8,128)} %copy-done.1) | copy-start | bytes 3145732
Sparse Core Ops, SparseCore 0:
  35.5 127.1 all-gather.1
